TPU v7x, 32 devices: a whole 2x2x4 slice. The times are simulated.
32 devices in a mesh: node: 8 (over z, x), rep: 4 (over y, core).
Axes of the slice: x: 2, y: 2, z: 4, core: 2. Of those that a mesh axis runs over, the one named last changes fastest.
Arguments:
- features: bfloat16 [163840, 256], P('node'), may hold values from -6 to 6
- w_in: bfloat16 [256, 256], replicated, may hold values from -0.375 to 0.375
- w_out: bfloat16 [256, 256], replicated, may hold values from -0.375 to 0.375
- pos_src: int32 [8, 4, 8, 2], P('node', 'rep'), may hold values from 0 to 159
- pos_dst: int32 [8, 4, 8, 2], P('node', 'rep'), may hold values from 0 to 159
- counts: int32 [8, 4, 8], P('node', 'rep'), may hold values from 1 to 2, as said below
- neg_blocks: int32 [8, 2], P('node'), may hold values from 0 to 159
- neg_pick: int32 [8, 4, 8, 2], P('node', 'rep'), may hold values from 0 to 15
Outputs:
- pos_scores: float32 [8, 4, 8, 2, 128], P('node', 'rep')
- neg_term: float32 [8, 4, 8, 2, 128], P('node', 'rep')
- loss: float32 [], replicated
Inputs may be any that keep to these rules, and one draw needn't show every extreme that they name: `counts`: each entry is at most 2; in every draw one owner receives 2 live slots from every device.
All inputs are finite; a program needn't handle non-finite values.
Results may differ from a plain program's by a relative error of at most 0.0027.
Values may be sent and summed in bfloat16 or wider, within the bound.
A program may use at most 192 MiB of HBM per device.

v0:
```python
import jax
import jax.numpy as jnp
from jax import lax
from jax.sharding import PartitionSpec as P

BLK = 128


def encode(rows_in, w_in, w_out):
    hidden = jax.nn.silu(jnp.dot(rows_in, w_in, preferred_element_type=jnp.float32)).astype(
        jnp.bfloat16
    )
    return jnp.dot(hidden, w_out, preferred_element_type=jnp.float32).astype(jnp.bfloat16)


def shards(features, w_in, w_out, pos_src, pos_dst, counts, neg_blocks, neg_pick):
    rows, width = features.shape
    owners = pos_dst.shape[2]
    slots = pos_dst.shape[3]
    embed = encode(features, w_in, w_out)
    blocks = embed.reshape(rows // BLK, BLK, width)
    asked_ids = pos_dst.reshape(owners, slots)
    reply = jnp.take(
        blocks, lax.all_to_all(asked_ids, "node", split_axis=0, concat_axis=0, tiled=True), axis=0
    )
    fetched = lax.all_to_all(reply, "node", split_axis=0, concat_axis=0, tiled=True)
    offered = jnp.take(blocks, neg_blocks.reshape(-1), axis=0)
    pool = lax.all_gather(offered, "node", axis=0, tiled=True)
    source = jnp.take(blocks, pos_src.reshape(-1), axis=0).reshape(owners, slots, BLK, width)
    cand = jnp.take(pool, neg_pick.reshape(-1), axis=0).reshape(owners, slots, BLK, width)
    scale = 1.0 / width**0.5
    raw_pos = (
        jnp.einsum("ocbd,ocbd->ocb", source, fetched, preferred_element_type=jnp.float32) * scale
    )
    scores = jnp.einsum("ocbd,ocsd->ocbs", source, cand, preferred_element_type=jnp.float32) * scale
    live = jnp.arange(slots, dtype=jnp.int32)[None, :] < counts.reshape(owners, 1)
    livex = live[..., None]
    pos_out = jnp.where(livex, raw_pos, 0.0)
    neg_out = jnp.where(livex, jnp.mean(jax.nn.softplus(scores), axis=-1), 0.0)
    pos_loss = jnp.sum(jnp.where(livex, jax.nn.softplus(-raw_pos), 0.0))
    totals = lax.psum(
        (pos_loss, jnp.sum(neg_out), jnp.sum(counts).astype(jnp.float32)), ("node", "rep")
    )
    loss = (totals[0] + totals[1]) / (BLK * totals[2])
    return (
        pos_out.reshape(1, 1, owners, slots, BLK),
        neg_out.reshape(1, 1, owners, slots, BLK),
        loss,
    )


def solution(mesh):
    return jax.shard_map(
        shards,
        mesh=mesh,
        in_specs=(
            P("node", None),
            P(),
            P(),
            P("node", "rep", None, None),
            P("node", "rep", None, None),
            P("node", "rep", None),
            P("node", None),
            P("node", "rep", None, None),
        ),
        out_specs=(P("node", "rep", None, None, None), P("node", "rep", None, None, None), P()),
        check_vma=False,
    )
```

profile of v0, /device:TPU:0, one launch (start us, length us, event | category | flops | bytes accessed | tf_op | source)
XLA Modules:
  0.0 137.5 jit_solution(16845520026060009428)
XLA Ops:
  7.2 1.4 %copy.25 = s32[8,1,2]{2,1,0:T(1,128)} copy(s32[8,1,2]{0,2,1:T(2,128)} %bitcast.44) | data formatting | bytes 128 | tf_op jit(solution)/shard_map/all_to_all | solution.py:24
  8.6 7.3 %all-to-all-start = ((s32[8,1,2]{2,1,0:T(1,128)}), s32[8,1,2]{2,1,0:T(1,128)S(1)}, u32[]{:S(2)}, u32[]{:S(2)}) async-start(s32[8,1,2]{2,1,0:T(1,128)} %copy.25), calls=%async_computation | async-start | bytes 8192 | tf_op jit(solution)/shard_map/all_to_all | solution.py:24
  15.8 0.0 all-gather.2.cloned.1.call-start
  15.9 0.7 fusion.8
  16.5 0.7 compare_and_fusion
  17.3 10.9 %convolution_convert_fusion = bf16[20480,256]{1,0:T(8,128)(2,1)} fusion(bf16[256,256]{1,0:T(8,128)(2,1)S(1)} %copy-done, bf16[20480,256]{1,0:T(8,128)(2,1)} %param.8, bf16[256,256]{1,0:T(8,128)(2,1)} %param.9), kind=kOutput, calls=%fused_computation.4 | convolution fusion | flops 5400166400 | bytes 21233664 | tf_op jit(solution)/shard_map/dot_general | solution.py:13
  28.2 4.5 %gather_fusion.2 = bf16[2,128,256]{2,1,0:T(8,128)(2,1)S(1)} fusion(bf16[160,128,256]{2,1,0:T(8,128)(2,1)} %bitcast.41, s32[1024]{0:T(1024)S(1)} %pad_clamp_fusion.1), kind=kCustom, calls=%fused_computation.2 | custom fusion | bytes 262152 | tf_op jit(solution)/shard_map/jit(_take)/gather | solution.py:27
  32.7 0.7 broadcast_select_fusion.3
  33.5 0.6 reduce_sum.39
  34.8 0.1 copy.24
  34.9 0.1 copy.26
  35.0 0.1 copy.27
  35.1 0.1 copy.29
  35.1 0.1 reshape.231
  35.2 4.6 %gather_fusion.1 = bf16[16,128,256]{2,1,0:T(8,128)(2,1)S(1)} fusion(bf16[160,128,256]{2,1,0:T(8,128)(2,1)} %bitcast.42, s32[1024]{0:T(1024)S(1)} %pad_clamp_fusion.2), kind=kCustom, calls=%fused_computation.1 | custom fusion | bytes 2097216 | tf_op jit(solution)/shard_map/jit(_take)/gather | solution.py:23
  39.8 1.1 broadcast_select_fusion
  41.0 6.0 %all-to-all-start.1 = ((bf16[8,2,128,256]{3,2,1,0:T(8,128)(2,1)}), bf16[8,2,128,256]{3,2,1,0:T(8,128)(2,1)S(1)}, u32[]{:S(2)}, u32[]{:S(2)}) async-start(bf16[8,2,128,256]{3,2,1,0:T(8,128)(2,1)} %broadcast_select_fusion), calls=%async_computation.1 | async-start | bytes 2097152 | tf_op jit(solution)/shard_map/all_to_all | solution.py:26
  46.9 0.1 copy.23
  47.0 0.1 copy.31
  47.1 0.1 copy.30
  47.2 0.1 reshape.215
  47.3 0.1 reshape.220
  47.4 4.6 %gather_fusion = bf16[16,128,256]{2,1,0:T(8,128)(2,1)S(1)} fusion(bf16[160,128,256]{2,1,0:T(8,128)(2,1)} %bitcast.43, s32[1024]{0:T(1024)S(1)} %pad_clamp_fusion.3), kind=kCustom, calls=%fused_computation | custom fusion | bytes 2097216 | tf_op jit(solution)/shard_map/jit(_take)/gather | solution.py:29
  52.0 0.1 iota_compare_fusion
  52.1 30.7 %all-gather.2.cloned.1.call-done = bf16[16,128,256]{2,1,0:T(8,128)(2,1)} async-done(((bf16[2,128,256]{2,1,0:T(8,128)(2,1)}), bf16[16,128,256]{2,1,0:T(8,128)(2,1)}) %all-gather.2.cloned.1.call-update) | async-done | bytes 1048592 | tf_op jit(solution)/shard_map/all_gather | solution.py:28
  82.8 1.8 %gather_fusion.3 = bf16[16,128,256]{2,1,0:T(8,128)(2,1)S(1)} fusion(bf16[16,128,256]{2,1,0:T(8,128)(2,1)} %all-gather.2.cloned.1.call-done, s32[1024]{0:T(1024)S(1)} %pad_clamp_fusion), kind=kCustom, calls=%fused_computation.3 | custom fusion | bytes 2097216 | tf_op jit(solution)/shard_map/jit(_take)/gather | solution.py:30
  84.7 0.5 fusion.4
  85.2 0.6 select_reduce_fusion
  85.9 0.5 fusion
  86.4 1.3 select_reduce_fusion.1
  89.0 0.7 bitcast_select_fusion
  89.7 38.6 %all-reduce = (f32[]{:T(128)}, f32[]{:T(128)}) all-reduce(f32[]{:T(128)S(6)} %add.94, f32[]{:T(128)S(6)} %convert_element_type.11), channel_id=1, replica_groups=mesh['node'=8,'rep'=4] {'node','rep'}, use_global_device_ids=true, to_apply=%region_2.3 | all-reduce | flops 2 | bytes 16 | tf_op jit(solution)/shard_map/psum | solution.py:41
  (21 shorter events, 0.1 us)
Async XLA Ops:
  7.2 10.1 %copy-start = (bf16[256,256]{1,0:T(8,128)(2,1)S(1)}, bf16[256,256]{1,0:T(8,128)(2,1)}, u32[]{:S(2)}) copy-start(bf16[256,256]{1,0:T(8,128)(2,1)} %param.10) | copy-start | bytes 393220
  8.6 26.3 %all-to-all-start = ((s32[8,1,2]{2,1,0:T(1,128)}), s32[8,1,2]{2,1,0:T(1,128)S(1)}, u32[]{:S(2)}, u32[]{:S(2)}) async-start(s32[8,1,2]{2,1,0:T(1,128)} %copy.25), calls=%async_computation | async-start | bytes 8192 | tf_op jit(solution)/shard_map/all_to_all | solution.py:24
  15.8 67.0 %all-gather.2.cloned.1.call-start = ((), (), s32[]{:S(2)}) async-start(), calls=%async_computation.2 | async-start | bytes 1179648 | tf_op jit(solution)/shard_map/all_gather | solution.py:28
  17.2 16.3 %copy-start.3 = (s32[1,1,8]{2,1,0:T(1,128)S(1)}, s32[1,1,8]{2,1,0:T(1,128)}, u32[]{:S(2)}) copy-start(s32[1,1,8]{2,1,0:T(1,128)} %param.13) | copy-start | bytes 100
  17.2 17.5 %copy-start.1 = (s32[1,1,8,2]{2,3,1,0:T(2,128)S(1)}, s32[1,1,8,2]{2,3,1,0:T(2,128)}, u32[]{:S(2)}) copy-start(s32[1,1,8,2]{2,3,1,0:T(2,128)} %param.11) | copy-start | bytes 196
  17.2 29.8 %copy-start.2 = (s32[1,1,8,2]{2,3,1,0:T(2,128)S(1)}, s32[1,1,8,2]{2,3,1,0:T(2,128)}, u32[]{:S(2)}) copy-start(s32[1,1,8,2]{2,3,1,0:T(2,128)} %param.15) | copy-start | bytes 196
  41.0 44.9 %all-to-all-start.1 = ((bf16[8,2,128,256]{3,2,1,0:T(8,128)(2,1)}), bf16[8,2,128,256]{3,2,1,0:T(8,128)(2,1)S(1)}, u32[]{:S(2)}, u32[]{:S(2)}) async-start(bf16[8,2,128,256]{3,2,1,0:T(8,128)(2,1)} %broadcast_select_fusion), calls=%async_computation.1 | async-start | bytes 2097152 | tf_op jit(solution)/shard_map/all_to_all | solution.py:26
Sparse Core Ops, SparseCore 0:
  33.6 49.2 all-gather.1
where the time goes:
time: 138 us
  blocking collectives  38.6 us (28%)
  waiting for transfers between devices  30.7 us (22%)
  between operations  18.6 us (13%)
  local copies, waits for them, and re-layouts  17.8 us (13%)
  starting transfers between devices  13.3 us (10%)
  matrix products  11.5 us (8%)
  other arithmetic  7.07 us (5%)
    psum x1, blocking collectives, shards(): lax.psum((pos_loss, jnp.sum(neg_out), jnp.sum(counts).astype(jnp.float32)...  38.6 us
    all_gather x1, waiting for transfers between devices, shards(): pool = lax.all_gather(offered, 'node', axis=0, tiled=True)  30.7 us
    dot_general x1, matrix products, encode(): jnp.dot(hidden, w_out, preferred_element_type=jnp.float32)  10.9 us
    all_to_all x1, starting transfers between devices, shards(): lax.all_to_all(asked_ids, 'node', split_axis=0, concat_axis=0, tiled=True)  7.28 us
    all_to_all x1, starting transfers between devices, shards(): lax.all_to_all(reply, 'node', split_axis=0, concat_axis=0, tiled=True)  5.95 us
    gather x1, local copies, waits for them, and re-layouts, shards(): jnp.take(blocks, pos_src.reshape(-1), axis=0)  4.61 us
    gather x1, local copies, waits for them, and re-layouts, shards(): jnp.take(blocks, lax.all_to_all(asked_ids, 'node', split_axis=0, concat_a...  4.59 us
    gather x1, local copies, waits for them, and re-layouts, shards(): offered = jnp.take(blocks, neg_blocks.reshape(-1), axis=0)  4.53 us
  transfers between devices with their start and end apart: 3, of which 1 were waited for; matrix products, arithmetic and copies ran while one was open for 24% of the time, Pallas kernels for 0%

commit v1 on v0

--- a/solution.py
+++ b/solution.py
@@ -17,16 +17,18 @@
     rows, width = features.shape
     owners = pos_dst.shape[2]
     slots = pos_dst.shape[3]
-    embed = encode(features, w_in, w_out)
-    blocks = embed.reshape(rows // BLK, BLK, width)
+    blocks = features.reshape(rows // BLK, BLK, width)
     asked_ids = pos_dst.reshape(owners, slots)
-    reply = jnp.take(
-        blocks, lax.all_to_all(asked_ids, "node", split_axis=0, concat_axis=0, tiled=True), axis=0
-    )
+    asked = lax.all_to_all(asked_ids, "node", split_axis=0, concat_axis=0, tiled=True)
+    offers = neg_blocks.size
+    wanted = jnp.concatenate([neg_blocks.reshape(-1), asked.reshape(-1), pos_src.reshape(-1)])
+    picked = jnp.take(blocks, wanted, axis=0)
+    picked = encode(picked.reshape(-1, width), w_in, w_out).reshape(-1, BLK, width)
+    offered = picked[:offers]
+    reply = picked[offers:offers + owners * slots].reshape(owners, slots, BLK, width)
+    source = picked[offers + owners * slots:].reshape(owners, slots, BLK, width)
     fetched = lax.all_to_all(reply, "node", split_axis=0, concat_axis=0, tiled=True)
-    offered = jnp.take(blocks, neg_blocks.reshape(-1), axis=0)
     pool = lax.all_gather(offered, "node", axis=0, tiled=True)
-    source = jnp.take(blocks, pos_src.reshape(-1), axis=0).reshape(owners, slots, BLK, width)
     cand = jnp.take(pool, neg_pick.reshape(-1), axis=0).reshape(owners, slots, BLK, width)
     scale = 1.0 / width**0.5
     raw_pos = (

time: 138 us -> 136 us (0.986)
  waiting for transfers between devices: 30.7 us -> 43.3 us
  matrix products: 11.5 us -> 3.57 us
  local copies, waits for them, and re-layouts: 17.8 us -> 11.7 us
  starting transfers between devices: 13.3 us -> 10.9 us
  other arithmetic: 7.07 us -> 9.1 us
    gather x3 -> x1, local copies, waits for them, and re-layouts: 13.7 us -> 4.67 us  [shards(): picked = jnp.take(blocks, wanted, axis=0)]
    dot_general x1, matrix products: 10.9 us -> 3.07 us  [encode(): jnp.dot(hidden, w_out, preferred_element_type=jnp.float32)]
    all_gather x1, waiting for transfers between devices: 30.7 us -> 37.9 us  [shards(): pool = lax.all_gather(offered, 'node', axis=0, tiled=True)]
    all_to_all x1, waiting for transfers between devices: 0.01 us -> 5.46 us  [shards(): lax.all_to_all(asked_ids, 'node', split_axis=0, concat_axis=0, tiled=True)]
    all_to_all x1, starting transfers between devices: 5.95 us -> 3.56 us  [shards(): lax.all_to_all(reply, 'node', split_axis=0, concat_axis=0, tiled=True)]
    slice x0 -> x2, local copies, waits for them, and re-layouts: none -> 1.83 us  [the longest x1 1.17 us: shards(): picked[offers:offers + owners * slots].reshape(owners, slots, BLK, width)]
    select_n x5 -> x2, other arithmetic: 2.54 us -> 4 us  [shards(): picked = jnp.take(blocks, wanted, axis=0)]
  transfers between devices with their start and end apart: 3 -> 3, of which waited for: 1 -> 2; matrix products, arithmetic and copies ran while one was open for 24% -> 4% of each run, Pallas kernels for 0% -> 0%
where the time goes in v1:
time: 136 us
  waiting for transfers between devices  43.3 us (32%)
  blocking collectives  38.5 us (28%)
  between operations  18.6 us (14%)
  local copies, waits for them, and re-layouts  11.7 us (9%)
  starting transfers between devices  10.9 us (8%)
  other arithmetic  9.1 us (7%)
  matrix products  3.57 us (3%)
    psum x1, blocking collectives, shards(): lax.psum((pos_loss, jnp.sum(neg_out), jnp.sum(counts).astype(jnp.float32)...  38.5 us
    all_gather x1, waiting for transfers between devices, shards(): pool = lax.all_gather(offered, 'node', axis=0, tiled=True)  37.9 us
    all_to_all x1, starting transfers between devices, shards(): lax.all_to_all(asked_ids, 'node', split_axis=0, concat_axis=0, tiled=True)  7.28 us
    all_to_all x1, waiting for transfers between devices, shards(): lax.all_to_all(asked_ids, 'node', split_axis=0, concat_axis=0, tiled=True)  5.46 us
    gather x1, local copies, waits for them, and re-layouts, shards(): picked = jnp.take(blocks, wanted, axis=0)  4.67 us
    select_n x2, other arithmetic, shards(): picked = jnp.take(blocks, wanted, axis=0)  4 us
    all_to_all x1, starting transfers between devices, shards(): lax.all_to_all(reply, 'node', split_axis=0, concat_axis=0, tiled=True)  3.56 us
    dot_general x1, matrix products, encode(): jnp.dot(hidden, w_out, preferred_element_type=jnp.float32)  3.07 us
  transfers between devices with their start and end apart: 3, of which 2 were waited for; matrix products, arithmetic and copies ran while one was open for 4% of the time, Pallas kernels for 0%

profile of v1, /device:TPU:0, one launch (start us, length us, event | category | flops | bytes accessed | tf_op | source)
XLA Modules:
  0.0 135.6 jit_solution(1148532893657339533)
XLA Ops:
  7.2 1.4 %copy.23 = s32[8,1,2]{2,1,0:T(1,128)} copy(s32[8,1,2]{0,2,1:T(2,128)} %bitcast.42) | data formatting | bytes 128 | tf_op jit(solution)/shard_map/all_to_all | solution.py:22
  8.6 7.3 %all-to-all-start = ((s32[8,1,2]{2,1,0:T(1,128)}), s32[8,1,2]{2,1,0:T(1,128)S(1)}, u32[]{:S(2)}, u32[]{:S(2)}) async-start(s32[8,1,2]{2,1,0:T(1,128)} %copy.23), calls=%async_computation | async-start | bytes 8192 | tf_op jit(solution)/shard_map/all_to_all | solution.py:22
  15.9 0.8 copy.24
  16.6 0.1 concatenate.44
  16.7 0.1 concatenate.40
  16.8 5.5 %all-to-all-done = s32[8,1,2]{2,1,0:T(1,128)S(1)} async-done(((s32[8,1,2]{2,1,0:T(1,128)}), s32[8,1,2]{2,1,0:T(1,128)S(1)}, u32[]{:S(2)}, u32[]{:S(2)}) %all-to-all-start) | async-done | bytes 96 | tf_op jit(solution)/shard_map/all_to_all | solution.py:22
  22.3 0.1 concatenate.43
  22.3 0.7 fusion.7
  23.1 0.5 broadcast.121
  23.6 0.7 reduce.9
  24.3 0.1 concatenate.39
  24.3 0.7 compare_and_fusion.1
  25.1 0.1 broadcast_bitcast_fusion
  25.2 4.7 %gather_fusion = bf16[34,128,256]{2,1,0:T(8,128)(2,1)S(1)} fusion(bf16[160,128,256]{2,1,0:T(8,128)(2,1)} %bitcast.38, s32[1024]{0:T(1024)S(1)} %pad_clamp_fusion.1), kind=kCustom, calls=%fused_computation | custom fusion | bytes 4456584 | tf_op jit(solution)/shard_map/jit(_take)/gather | solution.py:25
  29.8 3.3 %bitcast_select_fusion = bf16[4352,256]{1,0:T(8,128)(2,1)} fusion(bf16[34,128,256]{2,1,0:T(8,128)(2,1)S(1)} %gather_fusion, pred[4352]{0:T(1024)(128)(4,1)S(1)} %broadcast_bitcast_fusion), kind=kLoop, calls=%fused_computation.4 | loop fusion | flops 1114112 | bytes 4460800 | tf_op jit(solution)/shard_map/jit(_take)/select_n | solution.py:25
  33.1 3.1 %convolution_convert_fusion = bf16[4352,256]{1,0:T(8,128)(2,1)S(1)} fusion(bf16[256,256]{1,0:T(8,128)(2,1)S(1)} %copy-done, bf16[4352,256]{1,0:T(8,128)(2,1)} %bitcast_select_fusion, bf16[256,256]{1,0:T(8,128)(2,1)S(1)} %copy-done.2), kind=kOutput, calls=%fused_computation.2 | convolution fusion | flops 1147535360 | bytes 4718592 | tf_op jit(solution)/shard_map/dot_general | solution.py:13
  36.2 0.7 slice.24
  36.9 1.2 fusion.11
  38.1 3.6 %all-to-all-start.1 = ((bf16[8,2,128,256]{3,2,1,0:T(8,128)(2,1)}), bf16[8,2,128,256]{3,2,1,0:T(8,128)(2,1)S(1)}, u32[]{:S(2)}, u32[]{:S(2)}) async-start(bf16[8,2,128,256]{3,2,1,0:T(8,128)(2,1)} %bitcast.9), calls=%async_computation.1 | async-start | bytes 2097152 | tf_op jit(solution)/shard_map/all_to_all | solution.py:30
  41.7 0.1 copy.27
  41.7 0.1 reshape.260
  41.8 0.1 copy.26
  41.9 0.6 reduce_sum.39
  43.2 0.1 iota_compare_fusion
  43.3 37.9 %all-gather.2.cloned.1.call-done = bf16[16,128,256]{2,1,0:T(8,128)(2,1)} async-done(((bf16[2,128,256]{2,1,0:T(8,128)(2,1)}), bf16[16,128,256]{2,1,0:T(8,128)(2,1)}) %all-gather.2.cloned.1.call-update) | async-done | bytes 1048592 | tf_op jit(solution)/shard_map/all_gather | solution.py:31
  81.2 1.8 %gather_fusion.1 = bf16[16,128,256]{2,1,0:T(8,128)(2,1)S(1)} fusion(bf16[16,128,256]{2,1,0:T(8,128)(2,1)} %all-gather.2.cloned.1.call-done, s32[1024]{0:T(1024)S(1)} %pad_clamp_fusion), kind=kCustom, calls=%fused_computation.1 | custom fusion | bytes 2097216 | tf_op jit(solution)/shard_map/jit(_take)/gather | solution.py:32
  83.0 0.5 fusion.4
  83.5 0.6 select_reduce_fusion
  84.2 0.4 fusion
  84.5 1.3 select_reduce_fusion.1
  87.1 0.7 bitcast_select_fusion.1
  87.8 38.5 %all-reduce = (f32[]{:T(128)}, f32[]{:T(128)}) all-reduce(f32[]{:T(128)S(6)} %add.67, f32[]{:T(128)S(6)} %convert_element_type.11), channel_id=1, replica_groups=mesh['node'=8,'rep'=4] {'node','rep'}, use_global_device_ids=true, to_apply=%region_2.3 | all-reduce | flops 2 | bytes 16 | tf_op jit(solution)/shard_map/psum | solution.py:43
  (15 shorter events, 0.1 us)
Async XLA Ops:
  7.2 26.0 %copy-start = (bf16[256,256]{1,0:T(8,128)(2,1)S(1)}, bf16[256,256]{1,0:T(8,128)(2,1)}, u32[]{:S(2)}) copy-start(bf16[256,256]{1,0:T(8,128)(2,1)} %param.10) | copy-start | bytes 393220
  8.6 13.7 %all-to-all-start = ((s32[8,1,2]{2,1,0:T(1,128)}), s32[8,1,2]{2,1,0:T(1,128)S(1)}, u32[]{:S(2)}, u32[]{:S(2)}) async-start(s32[8,1,2]{2,1,0:T(1,128)} %copy.23), calls=%async_computation | async-start | bytes 8192 | tf_op jit(solution)/shard_map/all_to_all | solution.py:22
  15.8 65.3 %all-gather.2.cloned.1.call-start = ((), (), s32[]{:S(2)}) async-start(), calls=%async_computation.2 | async-start | bytes 1179648 | tf_op jit(solution)/shard_map/all_gather | solution.py:31
  29.8 3.3 %copy-start.2 = (bf16[256,256]{1,0:T(8,128)(2,1)S(1)}, bf16[256,256]{1,0:T(8,128)(2,1)}, u32[]{:S(2)}) copy-start(bf16[256,256]{1,0:T(8,128)(2,1)} %param.9) | copy-start | bytes 393220
  36.9 4.8 %copy-start.1 = (s32[1,1,8,2]{2,3,1,0:T(2,128)S(1)}, s32[1,1,8,2]{2,3,1,0:T(2,128)}, u32[]{:S(2)}) copy-start(s32[1,1,8,2]{2,3,1,0:T(2,128)} %param.15) | copy-start | bytes 196
  36.9 5.0 %copy-start.3 = (s32[1,1,8]{2,1,0:T(1,128)S(1)}, s32[1,1,8]{2,1,0:T(1,128)}, u32[]{:S(2)}) copy-start(s32[1,1,8]{2,1,0:T(1,128)} %param.13) | copy-start | bytes 100
  38.1 46.1 %all-to-all-start.1 = ((bf16[8,2,128,256]{3,2,1,0:T(8,128)(2,1)}), bf16[8,2,128,256]{3,2,1,0:T(8,128)(2,1)S(1)}, u32[]{:S(2)}, u32[]{:S(2)}) async-start(bf16[8,2,128,256]{3,2,1,0:T(8,128)(2,1)} %bitcast.9), calls=%async_computation.1 | async-start | bytes 2097152 | tf_op jit(solution)/shard_map/all_to_all | solution.py:30
Sparse Core Ops, SparseCore 0:
  37.0 44.1 all-gather.1

commit v2 on v0

v2 whole, which is shorter than its diff:
```python
import functools

import jax
import jax.numpy as jnp
from jax import lax
from jax.experimental import pallas as pl
from jax.experimental.pallas import tpu as pltpu
from jax.sharding import PartitionSpec as P

BLK = 128
LOADS = 8


def encode(rows_in, w_in, w_out):
    hidden = jax.nn.silu(jnp.dot(rows_in, w_in, preferred_element_type=jnp.float32)).astype(
        jnp.bfloat16
    )
    return jnp.dot(hidden, w_out, preferred_element_type=jnp.float32).astype(jnp.bfloat16)


def softplus(v):
    return jnp.maximum(v, 0.0) + jnp.log1p(jnp.exp(-jnp.abs(v)))


def partner(me, step, n):
    if n & (n - 1):
        return (me + step) % n
    out, bit = 0, 1
    while bit < n:
        out = out + ((me // bit + step // bit) % 2) * bit
        bit *= 2
    return out


def source_of(me, step, n):
    if n & (n - 1):
        return (me + n - step) % n
    return partner(me, step, n)


def mirror(step, n):
    return n - step if n & (n - 1) else step


def kernel(
    n, reps, slots, offers,
    src_ids, dst_ids, counts, neg_ids, picks, asks, features, w_in, w_out,
    pos_out, neg_out, loss_out,
    feat, heard, heard_s, reply, fetched, source, offer_own, pool, mine_sum, node_sums, rep_mine,
    rep_sums,
    load_sem, ask_send, ask_recv, local_sem, rep_send, rep_recv, off_send, off_recv,
    own_sem, fwd_send, fwd_recv, sum_send, sum_recv, all_send, all_recv,
):
    me = lax.axis_index("node")
    rep = lax.axis_index("rep")
    width = feat.shape[2]
    piece = feat.shape[0] // LOADS
    scale = 1.0 / width**0.5
    quarter = pool.shape[2]
    per_block = BLK // quarter

    def to_node(j):
        return {"node": j}

    def to_rep(j):
        return {"rep": j}

    def remote(src, dst, send, recv, where):
        return pltpu.make_async_remote_copy(
            src_ref=src, dst_ref=dst, send_sem=send, recv_sem=recv,
            device_id=where, device_id_type=pl.DeviceIdType.MESH,
        )

    loads = [
        pltpu.make_async_copy(
            features.at[pl.ds(s * piece, piece)], feat.at[pl.ds(s * piece, piece)], load_sem.at[s]
        )
        for s in range(LOADS)
    ]
    for load in loads:
        load.start()

    barrier = pltpu.get_barrier_semaphore()

    @pl.loop(1, n)
    def _(step):
        pl.semaphore_signal(
            barrier, inc=1, device_id=to_node(partner(me, step, n)),
            device_id_type=pl.DeviceIdType.MESH,
        )

    for step in range(1, reps):
        pl.semaphore_signal(
            barrier, inc=1, device_id=to_rep((rep + step) % reps),
            device_id_type=pl.DeviceIdType.MESH,
        )
    pl.semaphore_wait(barrier, n - 1 + reps - 1)

    def ask(step):
        to = partner(me, step, n)
        return remote(asks.at[to], heard.at[step], ask_send.at[step], ask_recv.at[step], to_node(to))

    @pl.loop(1, n)
    def _(i):
        ask(n - i).start()

    for load in loads:
        load.wait()

    wi = w_in[...]
    wo = w_out[...]

    def encoded(ids):
        rows = jnp.concatenate([feat[i] for i in ids], axis=0)
        return encode(rows, wi, wo)

    piece_at = pl.multiple_of((rep % per_block) * quarter, quarter)
    offer_own[...] = encode(feat[neg_ids[rep // per_block], pl.ds(piece_at, quarter)], wi, wo)

    own = encoded([dst_ids[me * slots + c] for c in range(slots)])
    reply[0] = own.reshape(slots, BLK, width)

    def offer(step):
        return remote(
            offer_own, pool.at[rep, me], off_send.at[step], off_recv.at[step],
            to_node(partner(me, step, n)),
        )

    @pl.loop(1, n)
    def _(i):
        offer(n - i).start()

    keep = pltpu.make_async_copy(offer_own, pool.at[rep, me], own_sem)
    keep.start()

    @pl.loop(1, n)
    def _(step):
        ask(step).wait()

    down = pltpu.make_async_copy(heard, heard_s, local_sem)
    down.start()
    down.wait()

    def answer(step):
        return remote(
            reply.at[step], fetched.at[step], rep_send.at[step], rep_recv.at[step],
            to_node(partner(me, step, n)),
        )

    @pl.loop(1, n)
    def _(i):
        step = n - i
        reply[step] = encoded(
            [heard_s[mirror(step, n), 0, c] for c in range(slots)]
        ).reshape(slots, BLK, width)

        @pl.when(i > 1)
        def _():
            answer(step + 1).start()

    @pl.loop(0, n)
    def _(o):
        source[o] = encoded([src_ids[o * slots + c] for c in range(slots)]).reshape(
            slots, BLK, width
        )

        @pl.when(o == 0)
        def _():
            answer(1).start()

    @pl.loop(1, n)
    def _(step):
        offer(step).wait()

    keep.wait()
    forwards = []
    for step in range(1, reps):
        to = (rep + step) % reps
        spot = pool.at[rep]
        forwards.append(remote(spot, spot, fwd_send.at[step - 1], fwd_recv.at[step - 1], to_rep(to)))
    for copy in forwards:
        copy.start()
    for copy in forwards:
        copy.wait()

    contract = (((1,), (1,)), ((), ()))

    def one_negative(o, c):
        pick = picks[o * slots + c]
        home = pick // offers
        first = (pick % offers) * per_block
        cand = jnp.concatenate([pool[first + h, home] for h in range(per_block)], axis=0)
        scores = scale * lax.dot_general(
            cand, source[o, c], contract, preferred_element_type=jnp.float32
        )
        term = jnp.sum(softplus(scores), axis=0, keepdims=True) * (1.0 / BLK)
        return jnp.where(c < counts[o], term, 0.0)

    def negatives(o, total):
        rows = [one_negative(o, c) for c in range(slots)]
        neg_out[o] = jnp.concatenate(rows, axis=0)
        return total + functools.reduce(jnp.add, rows)

    total = lax.fori_loop(0, n, negatives, jnp.zeros((1, BLK), jnp.float32))

    diagonal = lax.broadcasted_iota(jnp.int32, (BLK, BLK), 0) == lax.broadcasted_iota(
        jnp.int32, (BLK, BLK), 1
    )

    def positives(held, step, o, total):
        rows = []
        for c in range(slots):
            every = lax.dot_general(
                held[step, c], source[o, c], contract, preferred_element_type=jnp.float32
            )
            raw = scale * jnp.sum(jnp.where(diagonal, every, 0.0), axis=0, keepdims=True)
            live = c < counts[o]
            rows.append(jnp.where(live, raw, 0.0))
            total = total + jnp.where(live, softplus(-raw), 0.0)
        pos_out[o] = jnp.concatenate(rows, axis=0)
        return total

    total = positives(reply, 0, me, total)

    def arrived(i, total):
        step = n - i
        answer(step).wait()
        return positives(fetched, step, source_of(me, step, n), total)

    total = lax.fori_loop(1, n, arrived, total)

    asked = lax.fori_loop(0, n, lambda o, s: s + counts[o], jnp.int32(0))
    mine_sum[0:1] = total
    mine_sum[1:2] = jnp.full((1, BLK), asked.astype(jnp.float32))

    def tell(step):
        return remote(
            mine_sum, node_sums.at[step], sum_send.at[step], sum_recv.at[step],
            to_node(partner(me, step, n)),
        )

    @pl.loop(1, n)
    def _(i):
        tell(n - i).start()

    @pl.loop(1, n)
    def _(step):
        tell(step).wait()

    rep_mine[...] = lax.fori_loop(
        1, n, lambda step, sums: sums + node_sums[step], mine_sum[...]
    )
    tells = [
        remote(
            rep_mine, rep_sums.at[step], all_send.at[step], all_recv.at[step],
            to_rep((rep + step) % reps),
        )
        for step in range(1, reps)
    ]
    for copy in tells:
        copy.start()
    for copy in tells:
        copy.wait()
    sums = rep_mine[...]
    for step in range(1, reps):
        sums = sums + rep_sums[step]
    loss = jnp.sum(sums[0:1], axis=1, keepdims=True) / (BLK * sums[1:2, 0:1])
    loss_out[...] = loss


def shards(n, reps, features, w_in, w_out, pos_src, pos_dst, counts, neg_blocks, neg_pick):
    rows, width = features.shape
    owners = pos_dst.shape[2]
    slots = pos_dst.shape[3]
    offers = neg_blocks.shape[1]
    blocks = rows // BLK
    smem = pl.BlockSpec(memory_space=pltpu.SMEM)
    vmem = pl.BlockSpec(memory_space=pltpu.VMEM)
    dma = pltpu.SemaphoreType.DMA
    group = pltpu.VMEM((owners, slots, BLK, width), jnp.bfloat16)
    call = pl.pallas_call(
        functools.partial(kernel, n, reps, slots, offers),
        out_shape=(
            jax.ShapeDtypeStruct((owners, slots, BLK), jnp.float32),
            jax.ShapeDtypeStruct((owners, slots, BLK), jnp.float32),
            jax.ShapeDtypeStruct((1, 1), jnp.float32),
        ),
        in_specs=[smem] * 5 + [vmem, pl.BlockSpec(memory_space=pl.ANY), vmem, vmem],
        out_specs=(vmem, vmem, vmem),
        scratch_shapes=[
            pltpu.VMEM((blocks, BLK, width), jnp.bfloat16),
            pltpu.VMEM((n, 1, slots), jnp.int32),
            pltpu.SMEM((n, 1, slots), jnp.int32),
            group,
            group,
            group,
            pltpu.VMEM((offers * BLK // reps, width), jnp.bfloat16),
            pltpu.VMEM((reps, n, offers * BLK // reps, width), jnp.bfloat16),
            pltpu.VMEM((2, BLK), jnp.float32),
            pltpu.VMEM((n, 2, BLK), jnp.float32),
            pltpu.VMEM((2, BLK), jnp.float32),
            pltpu.VMEM((reps, 2, BLK), jnp.float32),
            dma((LOADS,)),
            dma((n,)),
            dma((n,)),
            dma,
            dma((n,)),
            dma((n,)),
            dma((n,)),
            dma((n,)),
            dma,
            dma((reps,)),
            dma((reps,)),
            dma((n,)),
            dma((n,)),
            dma((reps,)),
            dma((reps,)),
        ],
        compiler_params=pltpu.CompilerParams(
            collective_id=0, has_side_effects=True, vmem_limit_bytes=67043328
        ),
    )
    pos, neg, loss = call(
        pos_src.reshape(-1),
        pos_dst.reshape(-1),
        counts.reshape(-1),
        neg_blocks.reshape(-1),
        neg_pick.reshape(-1),
        pos_dst.reshape(owners, 1, slots),
        features.reshape(blocks, BLK, width),
        w_in,
        w_out,
    )
    shape = (1, 1, owners, slots, BLK)
    return pos.reshape(shape), neg.reshape(shape), loss.reshape(())


def solution(mesh):
    return jax.shard_map(
        functools.partial(shards, mesh.shape["node"], mesh.shape["rep"]),
        mesh=mesh,
        in_specs=(
            P("node", None),
            P(),
            P(),
            P("node", "rep", None, None),
            P("node", "rep", None, None),
            P("node", "rep", None),
            P("node", None),
            P("node", "rep", None, None),
        ),
        out_specs=(P("node", "rep", None, None, None), P("node", "rep", None, None, None), P()),
        check_vma=False,
    )
```

time: 138 us -> 61.6 us (0.45)
  Pallas kernels: 0 us -> 50.9 us
  blocking collectives: 38.6 us -> 0 us
  waiting for transfers between devices: 30.7 us -> 0 us
  between operations: 18.6 us -> 2.38 us
  starting transfers between devices: 13.3 us -> 0 us
  matrix products: 11.5 us -> 0 us
  local copies, waits for them, and re-layouts: 17.8 us -> 8.04 us
  other arithmetic: 7.07 us -> 0 us
    pallas_call x0 -> x1, Pallas kernels: none -> 50.9 us  [shards(): call(pos_src.reshape(-1), pos_dst.reshape(-1), counts.reshape(-1), neg_bl...]
    psum x1 -> x0, blocking collectives: 38.6 us -> none  [shards(): lax.psum((pos_loss, jnp.sum(neg_out), jnp.sum(counts).astype(jnp.float32)...]
    all_gather x1 -> x0, waiting for transfers between devices: 30.7 us -> none  [shards(): pool = lax.all_gather(offered, 'node', axis=0, tiled=True)]
    gather x4 -> x0, local copies, waits for them, and re-layouts: 15.6 us -> none  [the longest x1 4.61 us: shards(): jnp.take(blocks, pos_src.reshape(-1), axis=0)]
    all_to_all x2 -> x0, starting transfers between devices: 13.2 us -> none  [the longest x1 7.28 us: shards(): lax.all_to_all(asked_ids, 'node', split_axis=0, concat_axis=0, tiled=True)]
    dot_general x2 -> x0, matrix products: 11.5 us -> none  [the longest x1 10.9 us: encode(): jnp.dot(hidden, w_out, preferred_element_type=jnp.float32)]
    unnamed x10 -> x5, local copies, waits for them, and re-layouts: 0.19 us -> 4.85 us
    select_n x7 -> x0, other arithmetic: 3.22 us -> none  [the longest x2 1.4 us: shards(): offered = jnp.take(blocks, neg_blocks.reshape(-1), axis=0)]
  transfers between devices with their start and end apart: 3 -> 0, of which waited for: 1 -> 0; matrix products, arithmetic and copies ran while one was open for 24% -> 0% of each run, Pallas kernels for 0% -> 0%
where the time goes in v2:
time: 61.6 us; the launch traced here: 61.3 us
  Pallas kernels  50.9 us (83%)
  local copies, waits for them, and re-layouts  8.04 us (13%)
  between operations  2.38 us (4%)
    pallas_call x1, Pallas kernels, shards(): call(pos_src.reshape(-1), pos_dst.reshape(-1), counts.reshape(-1), neg_bl...  50.9 us
    unnamed x5, local copies, waits for them, and re-layouts  4.85 us
    reshape x1, local copies, waits for them, and re-layouts, shards(): pos_dst.reshape(owners, 1, slots)  1.34 us

profile of v2, /device:TPU:0, one launch (start us, length us, event | category | flops | bytes accessed | tf_op | source)
XLA Modules:
  0.0 61.3 jit_solution(17889004636963826278)
XLA Ops:
  0.6 0.8 %copy.15 = s32[1,1,8,2]{3,2,1,0:T(8,128)S(1)} copy(s32[1,1,8,2]{2,3,1,0:T(2,128)} %param.11) | data formatting | bytes 128 | tf_op args[3]
  1.4 0.6 reshape.36.src_ids
  2.0 0.8 %copy.17 = s32[1,1,8,2]{3,2,1,0:T(8,128)S(1)} copy(s32[1,1,8,2]{2,3,1,0:T(2,128)} %param.15) | data formatting | bytes 128 | tf_op args[7]
  2.7 0.7 %reshape.40.picks = s32[16]{0:T(128)} reshape(s32[1,1,8,2]{3,2,1,0:T(8,128)S(1)} %copy.17) | data formatting | bytes 128 | tf_op jit(solution)/shard_map/reshape | solution.py:328
  3.4 1.3 %copy.18.asks = s32[8,1,2]{2,1,0:T(1,128)} copy(s32[8,1,2]{0,2,1:T(2,128)} %bitcast.16) | data formatting | bytes 128 | tf_op jit(solution)/shard_map/reshape | solution.py:329
  4.7 0.8 %copy.16 = s32[1,1,8,2]{3,2,1,0:T(8,128)S(1)} copy(s32[1,1,8,2]{2,3,1,0:T(2,128)} %param.12) | data formatting | bytes 128 | tf_op args[4]
  5.5 0.6 reshape.37.dst_ids
  6.1 50.9 %shard_map.103 = (f32[8,2,128]{2,1,0:T(2,128)}, f32[8,2,128]{2,1,0:T(2,128)}, f32[1,1]{1,0:T(1,128)}) custom-call(s32[16]{0:T(128)} %reshape.36.src_ids, s32[16]{0:T(128)} %reshape.37.dst_ids, s32[8]{0:T(128)} %bitcast.17, s32[2]{0:T(128)} %bitcast.18, s32[16]{0:T(128)} %reshape.40.picks, s32[8,1,2]{2,1,0:T(1,128)} %copy.18.asks, ...), custom_call_target="tpu_custom_call" | custom-call | tf_op jit(solution)/shard_map/pallas_call | solution.py:323
  56.9 1.3 %copy.22 = f32[1,1,8,2,128]{4,3,2,1,0:T(2,128)} copy(f32[1,1,8,2,128]{4,3,2,1,0:T(2,128)} %bitcast.15) | data formatting | bytes 16384
  58.2 1.3 %copy.23 = f32[1,1,8,2,128]{4,3,2,1,0:T(2,128)} copy(f32[1,1,8,2,128]{4,3,2,1,0:T(2,128)} %bitcast.14) | data formatting | bytes 16384

commit v3 on v2

--- a/solution.py
+++ b/solution.py
@@ -49,14 +49,15 @@
     feat, heard, heard_s, reply, fetched, source, offer_own, pool, mine_sum, node_sums, rep_mine,
     rep_sums,
     load_sem, ask_send, ask_recv, local_sem, rep_send, rep_recv, off_send, off_recv,
-    own_sem, fwd_send, fwd_recv, sum_send, sum_recv, all_send, all_recv,
+    own_sem, near_send, near_recv, fwd_send, fwd_recv, sum_send, sum_recv, all_send, all_recv,
 ):
     me = lax.axis_index("node")
     rep = lax.axis_index("rep")
     width = feat.shape[2]
     piece = feat.shape[0] // LOADS
     scale = 1.0 / width**0.5
-    quarter = pool.shape[2]
+    lows, highs, quarter = pool.shape[1:4]
+    low, high = me % lows, me // lows
     per_block = BLK // quarter
 
     def to_node(j):
@@ -98,7 +99,7 @@
 
     def ask(step):
         to = partner(me, step, n)
-        return remote(asks.at[to], heard.at[step], ask_send.at[step], ask_recv.at[step], to_node(to))
+        return remote(asks, heard.at[step], ask_send.at[step], ask_recv.at[step], to_node(to))
 
     @pl.loop(1, n)
     def _(i):
@@ -117,20 +118,20 @@
     piece_at = pl.multiple_of((rep % per_block) * quarter, quarter)
     offer_own[...] = encode(feat[neg_ids[rep // per_block], pl.ds(piece_at, quarter)], wi, wo)
 
-    own = encoded([dst_ids[me * slots + c] for c in range(slots)])
+    own = encoded([dst_ids[c, me] for c in range(slots)])
     reply[0] = own.reshape(slots, BLK, width)
 
     def offer(step):
         return remote(
-            offer_own, pool.at[rep, me], off_send.at[step], off_recv.at[step],
-            to_node(partner(me, step, n)),
-        )
-
-    @pl.loop(1, n)
+            offer_own, pool.at[rep, low, high], off_send.at[step], off_recv.at[step],
+            to_node(partner(high, step, highs) * lows + low),
+        )
+
+    @pl.loop(1, highs)
     def _(i):
-        offer(n - i).start()
-
-    keep = pltpu.make_async_copy(offer_own, pool.at[rep, me], own_sem)
+        offer(highs - i).start()
+
+    keep = pltpu.make_async_copy(offer_own, pool.at[rep, low, high], own_sem)
     keep.start()
 
     @pl.loop(1, n)
@@ -151,7 +152,7 @@
     def _(i):
         step = n - i
         reply[step] = encoded(
-            [heard_s[mirror(step, n), 0, c] for c in range(slots)]
+            [heard_s[mirror(step, n), c, me] for c in range(slots)]
         ).reshape(slots, BLK, width)
 
         @pl.when(i > 1)
@@ -160,7 +161,7 @@
 
     @pl.loop(0, n)
     def _(o):
-        source[o] = encoded([src_ids[o * slots + c] for c in range(slots)]).reshape(
+        source[o] = encoded([src_ids[c, o] for c in range(slots)]).reshape(
             slots, BLK, width
         )
 
@@ -168,11 +169,18 @@
         def _():
             answer(1).start()
 
-    @pl.loop(1, n)
+    @pl.loop(1, highs)
     def _(step):
         offer(step).wait()
 
     keep.wait()
+    for step in range(1, lows):
+        spot = pool.at[rep, low]
+        across = remote(
+            spot, spot, near_send, near_recv, to_node(high * lows + (low + step) % lows)
+        )
+        across.start()
+        across.wait()
     forwards = []
     for step in range(1, reps):
         to = (rep + step) % reps
@@ -186,10 +194,10 @@
     contract = (((1,), (1,)), ((), ()))
 
     def one_negative(o, c):
-        pick = picks[o * slots + c]
+        pick = picks[c, o]
         home = pick // offers
         first = (pick % offers) * per_block
-        cand = jnp.concatenate([pool[first + h, home] for h in range(per_block)], axis=0)
+        cand = jnp.concatenate([pool[first + h, home % lows, home // lows] for h in range(per_block)], axis=0)
         scores = scale * lax.dot_general(
             cand, source[o, c], contract, preferred_element_type=jnp.float32
         )
@@ -274,10 +282,15 @@
     slots = pos_dst.shape[3]
     offers = neg_blocks.shape[1]
     blocks = rows // BLK
+    lows = 1 if n % 2 else 2
     smem = pl.BlockSpec(memory_space=pltpu.SMEM)
     vmem = pl.BlockSpec(memory_space=pltpu.VMEM)
     dma = pltpu.SemaphoreType.DMA
     group = pltpu.VMEM((owners, slots, BLK, width), jnp.bfloat16)
+
+    def by_slot(ids):
+        return jnp.swapaxes(ids, 2, 3).reshape(slots, owners)
+
     call = pl.pallas_call(
         functools.partial(kernel, n, reps, slots, offers),
         out_shape=(
@@ -289,13 +302,13 @@
         out_specs=(vmem, vmem, vmem),
         scratch_shapes=[
             pltpu.VMEM((blocks, BLK, width), jnp.bfloat16),
-            pltpu.VMEM((n, 1, slots), jnp.int32),
-            pltpu.SMEM((n, 1, slots), jnp.int32),
+            pltpu.VMEM((n, slots, owners), jnp.int32),
+            pltpu.SMEM((n, slots, owners), jnp.int32),
             group,
             group,
             group,
             pltpu.VMEM((offers * BLK // reps, width), jnp.bfloat16),
-            pltpu.VMEM((reps, n, offers * BLK // reps, width), jnp.bfloat16),
+            pltpu.VMEM((reps, lows, n // lows, offers * BLK // reps, width), jnp.bfloat16),
             pltpu.VMEM((2, BLK), jnp.float32),
             pltpu.VMEM((n, 2, BLK), jnp.float32),
             pltpu.VMEM((2, BLK), jnp.float32),
@@ -308,6 +321,8 @@
             dma((n,)),
             dma((n,)),
             dma((n,)),
+            dma,
+            dma,
             dma,
             dma((reps,)),
             dma((reps,)),
@@ -321,12 +336,12 @@
         ),
     )
     pos, neg, loss = call(
-        pos_src.reshape(-1),
-        pos_dst.reshape(-1),
+        by_slot(pos_src),
+        by_slot(pos_dst),
         counts.reshape(-1),
         neg_blocks.reshape(-1),
-        neg_pick.reshape(-1),
-        pos_dst.reshape(owners, 1, slots),
+        by_slot(neg_pick),
+        by_slot(pos_dst),
         features.reshape(blocks, BLK, width),
         w_in,
         w_out,

time: 61.6 us -> 53.4 us (0.87)
  local copies, waits for them, and re-layouts: 8.04 us -> 2.59 us
  Pallas kernels: 50.9 us -> 48.1 us
    reshape x4 -> x0, local copies, waits for them, and re-layouts: 3.19 us -> none  [the longest x1 1.34 us: shards(): pos_dst.reshape(owners, 1, slots)]
    pallas_call x1, Pallas kernels: 50.9 us -> 48.1 us  [shards(): call(by_slot(pos_src), by_slot(pos_dst), counts.reshape(-1), neg_blocks.r...]
    unnamed x5 -> x2, local copies, waits for them, and re-layouts: 4.85 us -> 2.59 us
where the time goes in v3:
time: 53.4 us; the launch traced here: 53.1 us
  Pallas kernels  48.1 us (90%)
  local copies, waits for them, and re-layouts  2.59 us (5%)
  between operations  2.4 us (4%)
    pallas_call x1, Pallas kernels, shards(): call(by_slot(pos_src), by_slot(pos_dst), counts.reshape(-1), neg_blocks.r...  48.1 us
    unnamed x2, local copies, waits for them, and re-layouts  2.59 us

profile of v3, /device:TPU:0, one launch (start us, length us, event | category | flops | bytes accessed | tf_op | source)
XLA Modules:
  0.0 53.1 jit_solution(15813351079653153227)
XLA Ops:
  0.6 48.1 %shard_map.103 = (f32[8,2,128]{2,1,0:T(2,128)}, f32[8,2,128]{2,1,0:T(2,128)}, f32[1,1]{1,0:T(1,128)}) custom-call(s32[2,8]{1,0:T(2,128)} %bitcast.20, s32[2,8]{1,0:T(2,128)} %bitcast.18, s32[8]{0:T(128)} %bitcast.22, s32[2]{0:T(128)} %bitcast.23, s32[2,8]{1,0:T(2,128)} %bitcast.21, s32[2,8]{1,0:T(2,128)} %bitcast.19, bf16[160,128,256]{2,1,0:T(8,128)(2,1)} %bitcast.15, ...), custom_call_target="tpu_custom_call" | custom-call | tf_op jit(solution)/shard_map/pallas_call | solution.py:338
  48.8 1.3 %copy.14 = f32[1,1,8,2,128]{4,3,2,1,0:T(2,128)} copy(f32[1,1,8,2,128]{4,3,2,1,0:T(2,128)} %bitcast.17) | data formatting | bytes 16384
  50.1 1.3 %copy.15 = f32[1,1,8,2,128]{4,3,2,1,0:T(2,128)} copy(f32[1,1,8,2,128]{4,3,2,1,0:T(2,128)} %bitcast.16) | data formatting | bytes 16384
